TPU v7x, 8 devices: a whole 2x2x1 slice. The times are simulated.
8 devices in a mesh: side: 2 (over z, y), rep: 4 (over x, core).
Axes of the slice: x: 2, y: 2, z: 1, core: 2. Of those that a mesh axis runs over, the one named last changes fastest.
Arguments:
- w_up: float32 [2, 1, 3072, 8192], P('side', None, 'rep')
- w_down: float32 [2, 1, 8192, 3072], P('side', None, None, 'rep')
- g_up: float32 [2, 1, 3072, 8192], P('side', None, 'rep')
- g_down: float32 [2, 1, 8192, 3072], P('side', None, None, 'rep')
- learn_rate: float32 [], replicated
- prompts: bfloat16 [2, 8192, 3072], P('side', 'rep')
- prompt_lens: int32 [4], P('rep')
Outputs:
- output 1: float32 [2, 1, 3072, 8192], P('side', None, 'rep')
- output 2: float32 [2, 1, 8192, 3072], P('side', None, None, 'rep')
- output 3: bfloat16 [2, 8192, 3072], P('side', 'rep')
All inputs are finite; a program needn't handle non-finite values.
Results may differ from a plain program's by a relative error of at most 0.001.
Values are sent between devices in bfloat16 or wider.
A program may use at most 1 GiB of HBM per device.

v0:
```python
import jax
import jax.numpy as jnp
from jax import lax
from jax.sharding import PartitionSpec as P


def solution(mesh):
    side_devs = mesh.shape["side"]
    tp_ways = side_devs // 2
    cross_perm = [(src_pos, src_pos + tp_ways) for src_pos in range(tp_ways)]
    up_spec = P("side", None, "rep", None)
    down_spec = P("side", None, None, "rep")
    act_spec = P("side", "rep", None)

    def device_step(w_up, w_down, g_up, g_down, learn_rate, prompts, prompt_lens):
        new_up = w_up - learn_rate * g_up
        new_down = w_down - learn_rate * g_down
        up_sent = lax.ppermute(new_up[0].astype(jnp.bfloat16), "side", cross_perm)
        down_sent = lax.ppermute(new_down[0].astype(jnp.bfloat16), "side", cross_perm)
        up_full = lax.all_gather(up_sent, "rep", axis=1, tiled=True)
        down_full = lax.all_gather(down_sent, "rep", axis=2, tiled=True)
        side_idx = lax.axis_index("side")
        is_gen = side_idx >= tp_ways
        tokens = prompts.shape[1]
        d_piece = prompts.shape[2]
        if tp_ways > 1:
            pieces = lax.all_gather(prompts[0], "side", axis=0)
            hidden = jnp.transpose(pieces[tp_ways:], (1, 0, 2)).reshape(tokens, tp_ways * d_piece)
        else:
            hidden = prompts[0]
        for layer_idx in range(up_full.shape[0]):
            pre_act = jnp.dot(hidden, up_full[layer_idx], preferred_element_type=jnp.float32)
            act_bf = jax.nn.gelu(pre_act, approximate=True).astype(jnp.bfloat16)
            part_sum = jnp.dot(act_bf, down_full[layer_idx], preferred_element_type=jnp.float32)
            if tp_ways > 1:
                part_sum = lax.psum(jnp.where(is_gen, part_sum, 0.0), "side")
            hidden = (hidden.astype(jnp.float32) + part_sum).astype(jnp.bfloat16)
        keep_mask = jnp.arange(tokens)[:, None] < prompt_lens[0]
        tp_idx = jnp.maximum(side_idx - tp_ways, 0)
        own_cols = lax.dynamic_slice_in_dim(hidden, tp_idx * d_piece, d_piece, axis=1)
        out_block = jnp.where(keep_mask & is_gen, own_cols, jnp.zeros_like(own_cols))
        return new_up, new_down, out_block[None]

    mapped = jax.shard_map(
        device_step,
        mesh=mesh,
        in_specs=(up_spec, down_spec, up_spec, down_spec, P(), act_spec, P("rep")),
        out_specs=(up_spec, down_spec, act_spec),
        check_vma=False,
    )
    return mapped
```

profile of v0, /device:TPU:4, one launch (start us, length us, event | category | flops | bytes accessed | tf_op | source)
XLA Modules:
  0.0 1033.2 jit_solution(998974385637492926)
XLA Ops:
  7.2 0.0 all-gather.3.cloned.1.call-start
  7.9 25.7 %convert_bitcast_fusion.1 = (bf16[1,768,8192]{2,1,0:T(8,128)(2,1)S(1)}, f32[1,1,768,8192]{3,2,1,0:T(8,128)}) fusion(f32[1,1,768,8192]{3,2,1,0:T(8,128)} %param.7, f32[1,1,768,8192]{3,2,1,0:T(8,128)} %param.9, f32[]{:T(128)S(6)} %copy.10), kind=kLoop, calls=%fused_computation.19 | loop fusion | flops 18874368 | bytes 88080384 | tf_op jit(solution)/shard_map/convert_element_type | solution.py:18
  33.5 1.3 collective-permute-start
  34.8 272.7 %collective-permute-done = bf16[1,768,8192]{2,1,0:T(8,128)(2,1)} collective-permute-done((bf16[1,768,8192]{2,1,0:T(8,128)(2,1)S(1)}, bf16[1,768,8192]{2,1,0:T(8,128)(2,1)}, u32[]{:S(2)}, u32[]{:S(2)}) %collective-permute-start) | collective-permute-done | bytes 12582944 | tf_op jit(solution)/shard_map/ppermute | solution.py:18
  307.5 0.0 all-gather.3.cloned.1.call-update
  307.5 0.0 all-gather.5.cloned.1.call-start
  307.6 25.9 %convert_bitcast_fusion = (bf16[1,8192,768]{2,1,0:T(8,128)(2,1)S(1)}, f32[1,1,8192,768]{3,2,1,0:T(8,128)}) fusion(f32[1,1,8192,768]{3,2,1,0:T(8,128)} %param.8, f32[1,1,8192,768]{3,2,1,0:T(8,128)} %param.10, f32[]{:T(128)S(6)} %copy.10), kind=kLoop, calls=%fused_computation.18 | loop fusion | flops 18874368 | bytes 88080384 | tf_op jit(solution)/shard_map/convert_element_type | solution.py:19
  333.5 1.3 collective-permute-start.1
  334.8 271.9 %collective-permute-done.1 = bf16[1,8192,768]{2,1,0:T(8,128)(2,1)} collective-permute-done((bf16[1,8192,768]{2,1,0:T(8,128)(2,1)S(1)}, bf16[1,8192,768]{2,1,0:T(8,128)(2,1)}, u32[]{:S(2)}, u32[]{:S(2)}) %collective-permute-start.1) | collective-permute-done | bytes 12582944 | tf_op jit(solution)/shard_map/ppermute | solution.py:19
  606.7 0.0 all-gather.5.cloned.1.call-update
  607.4 0.6 fusion.19
  608.0 0.0 all-gather.3.cloned.1.call-done
  608.0 0.0 copy-start
  608.0 134.6 %fusion.7 = bf16[2048,8192]{0,1:T(8,128)(2,1)} fusion(bf16[1,3072,8192]{2,1,0:T(8,128)(2,1)} %all-gather.3.cloned.1.call-done, bf16[1,2048,3072]{2,1,0:T(8,128)(2,1)} %param.12), kind=kOutput, calls=%fused_computation.8 | convolution fusion | flops 103230210048 | bytes 96468992 | tf_op jit(solution)/shard_map/dot_general | solution.py:32
  742.6 162.0 %all-gather.5.cloned.1.call-done = bf16[1,8192,3072]{2,1,0:T(8,128)(2,1)} async-done(((bf16[1,8192,768]{2,1,0:T(8,128)(2,1)}), bf16[1,8192,3072]{2,1,0:T(8,128)(2,1)}) %all-gather.5.cloned.1.call-update) | async-done | bytes 50331664 | tf_op jit(solution)/shard_map/all_gather | solution.py:21
  904.6 0.0 copy-done
  904.6 121.8 %select_bitcast_fusion = bf16[1,2048,3072]{2,1,0:T(8,128)(2,1)} fusion(pred[2048]{0:T(1024)(128)(4,1)S(1)} %copy-done, bf16[2048,8192]{0,1:T(8,128)(2,1)} %fusion.7, bf16[1,8192,3072]{2,1,0:T(8,128)(2,1)} %all-gather.5.cloned.1.call-done, bf16[1,2048,3072]{2,1,0:T(8,128)(2,1)} %param.12), kind=kOutput, calls=%fused_computation.17 | convolution fusion | flops 103104380928 | bytes 109053952 | tf_op jit(solution)/shard_map/dot_general | solution.py:34
Async XLA Ops:
  7.2 600.8 %all-gather.3.cloned.1.call-start = ((), (), s32[]{:S(2)}) async-start(), calls=%async_computation | async-start | bytes 62914560 | tf_op jit(solution)/shard_map/all_gather | solution.py:20
  33.5 274.0 %collective-permute-start = (bf16[1,768,8192]{2,1,0:T(8,128)(2,1)S(1)}, bf16[1,768,8192]{2,1,0:T(8,128)(2,1)}, u32[]{:S(2)}, u32[]{:S(2)}) collective-permute-start(bf16[1,768,8192]{2,1,0:T(8,128)(2,1)S(1)} %get-tuple-element.5), channel_id=1, source_target_pairs={{0,4},{1,5},{2,6},{3,7}} | collective-permute-start | bytes 37748744 | tf_op jit(solution)/shard_map/ppermute | solution.py:18
  307.5 597.0 %all-gather.5.cloned.1.call-start = ((), (), s32[]{:S(2)}) async-start(), calls=%async_computation.1 | async-start | bytes 62914560 | tf_op jit(solution)/shard_map/all_gather | solution.py:21
  333.5 273.2 %collective-permute-start.1 = (bf16[1,8192,768]{2,1,0:T(8,128)(2,1)S(1)}, bf16[1,8192,768]{2,1,0:T(8,128)(2,1)}, u32[]{:S(2)}, u32[]{:S(2)}) collective-permute-start(bf16[1,8192,768]{2,1,0:T(8,128)(2,1)S(1)} %get-tuple-element.3), channel_id=1, source_target_pairs={{0,4},{1,5},{2,6},{3,7}} | collective-permute-start | bytes 37748744 | tf_op jit(solution)/shard_map/ppermute | solution.py:19
  608.0 296.6 %copy-start = (pred[2048]{0:T(1024)(128)(4,1)S(1)}, pred[2048]{0:T(1024)(128)(4,1)}, u32[]{:S(2)}) copy-start(pred[2048]{0:T(1024)(128)(4,1)} %fusion.19) | copy-start | bytes 6148
Sparse Core Ops, SparseCore 0:
  307.7 295.4 all-gather.2
  606.9 297.6 all-gather.4
where the time goes:
time: 1040 us; the launch traced here: 1030 us
  waiting for transfers between devices  707 us (68%)
  matrix products  256 us (25%)
  other arithmetic  52.2 us (5%)
  between operations  15.4 us (1%)
    ppermute x1, waiting for transfers between devices, device_step(): up_sent = lax.ppermute(new_up[0].astype(jnp.bfloat16), 'side', cross_perm)  273 us
    ppermute x1, waiting for transfers between devices, device_step(): lax.ppermute(new_down[0].astype(jnp.bfloat16), 'side', cross_perm)  272 us
    all_gather x1, waiting for transfers between devices, device_step(): down_full = lax.all_gather(down_sent, 'rep', axis=2, tiled=True)  162 us
    dot_general x1, matrix products, device_step(): jnp.dot(hidden, up_full[layer_idx], preferred_element_type=jnp.float32)  135 us
    dot_general x1, matrix products, device_step(): jnp.dot(act_bf, down_full[layer_idx], preferred_element_type=jnp.float32)  122 us
    convert_element_type x1, other arithmetic, device_step(): new_down[0].astype(jnp.bfloat16)  25.9 us
    convert_element_type x1, other arithmetic, device_step(): up_sent = lax.ppermute(new_up[0].astype(jnp.bfloat16), 'side', cross_perm)  25.7 us
  transfers between devices with their start and end apart: 4, of which 3 were waited for; matrix products, arithmetic and copies ran while one was open for 16% of the time, Pallas kernels for 0%

commit v1 on v0

v1 whole, which is shorter than its diff:
```python
import functools

import jax
import jax.numpy as jnp
from jax import lax
from jax.experimental import pallas as pl
from jax.experimental.pallas import tpu as pltpu
from jax.sharding import PartitionSpec as P

MESH = pl.DeviceIdType.MESH
CHUNK = 256
HEAD = 3
ROWS = 512
COLS = 768
OUT_ROWS = 256


def stream_kernel(
    up_ref, down_ref, up_head, down_head, x_hbm,
    y_hbm, up_all, down_all,
    x_ref, total, up_slot, down_slot, up_bounce, down_bounce, y_stage,
    send_y, recv_y, send_x, recv_x, send_d, recv_d, send_f, recv_f,
    load_sem, head_sem, x_sem, y_sem,
):
    side = lax.axis_index("side")
    me = lax.axis_index("rep")
    mate = me + 1 - 2 * lax.rem(me, 2)
    across = lax.rem(me + 2, 4)
    width = up_ref.shape[0]
    count = up_ref.shape[1] // CHUNK
    tokens = x_ref.shape[0]

    barrier = pltpu.get_barrier_semaphore()
    for peer in ((side, mate), (side, across), (1 - side, me)):
        pl.semaphore_signal(barrier, inc=1, device_id=peer, device_id_type=MESH)
    pl.semaphore_wait(barrier, 3)

    def wide(c):
        return pl.ds(pl.multiple_of(c * CHUNK, CHUNK), CHUNK)

    def piece(q):
        return pl.ds(pl.multiple_of(q * width, width), width)

    def remote(src, dst, send, recv, peer):
        return pltpu.make_async_remote_copy(
            src_ref=src, dst_ref=dst, send_sem=send, recv_sem=recv, device_id=peer, device_id_type=MESH
        )

    def down_link(c):
        return (
            remote(up_ref.at[:, wide(c)], up_all.at[c, piece(me), :], send_y.at[0, c], recv_y.at[0, c], (1, me)),
            remote(down_ref.at[wide(c), :], down_all.at[c, :, piece(me)], send_y.at[1, c], recv_y.at[1, c], (1, me)),
        )

    def relay(c, q, send, recv, peer):
        up_part = up_all.at[c, piece(q), :]
        down_part = down_all.at[c, :, piece(q)]
        return (
            remote(up_part, up_part, send.at[0, c], recv.at[0, c], (1, peer)),
            remote(down_part, down_part, send.at[1, c], recv.at[1, c], (1, peer)),
        )

    def to_across(c):
        return relay(c, me, send_x, recv_x, across)

    def to_mate(c):
        return relay(c, me, send_d, recv_d, mate)

    def forward(c):
        return relay(c, across, send_f, recv_f, mate)

    def loads(c):
        slot = lax.rem(c, 2)
        return (
            pltpu.make_async_copy(up_all.at[c], up_slot.at[slot], load_sem.at[0, slot]),
            pltpu.make_async_copy(down_all.at[c], down_slot.at[slot], load_sem.at[1, slot]),
        )

    @pl.when(side == 0)
    def _():
        def send(c, carry):
            for copy in down_link(c):
                copy.start()

            @pl.when(c >= HEAD + 2)
            def _():
                for copy in down_link(c - 2):
                    copy.wait_send()

            return carry

        lax.fori_loop(HEAD, count, send, 0)
        for c in (count - 2, count - 1):
            for copy in down_link(c):
                copy.wait_send()

    @pl.when(side == 1)
    def _():
        x_copy = pltpu.make_async_copy(x_hbm, x_ref, x_sem)
        heads = (
            pltpu.make_async_copy(up_head, up_bounce, head_sem.at[0]),
            pltpu.make_async_copy(down_head, down_bounce, head_sem.at[1]),
        )
        for copy in heads:
            copy.start()
        for copy in heads:
            copy.wait()
        x_copy.start()
        places = []
        for c in range(HEAD):
            part = slice(c * CHUNK, (c + 1) * CHUNK)
            places.append(
                pltpu.make_async_copy(up_bounce.at[:, part], up_all.at[c, piece(me), :], send_y.at[0, c])
            )
            places.append(
                pltpu.make_async_copy(down_bounce.at[part, :], down_all.at[c, :, piece(me)], send_y.at[1, c])
            )
        for copy in places:
            copy.start()
        for copy in places:
            copy.wait()
        total[...] = jnp.zeros_like(total)
        x_copy.wait()

        def compute(slot):
            def block(t, carry):
                rows = pl.ds(pl.multiple_of(t * ROWS, ROWS), ROWS)
                pre = jnp.dot(x_ref[rows, :], up_slot[slot], preferred_element_type=jnp.float32)
                act = jax.nn.gelu(pre, approximate=True).astype(jnp.bfloat16)
                for n in range(0, total.shape[1], COLS):
                    total[rows, n : n + COLS] += jnp.dot(
                        act, down_slot[slot, :, n : n + COLS], preferred_element_type=jnp.float32
                    )
                return carry

            lax.fori_loop(0, tokens // ROWS, block, 0)

        def turn(c, carry):
            @pl.when(c < count)
            def _():
                @pl.when(c >= HEAD)
                def _():
                    for copy in down_link(c):
                        copy.wait_recv()

                for copy in to_across(c) + to_mate(c):
                    copy.start()

            @pl.when(c >= 2)
            def _():
                for copy in loads(c - 2):
                    copy.wait()
                compute(lax.rem(c, 2))

            @pl.when((c >= 1) & (c <= count))
            def _():
                for copy in to_across(c - 1):
                    copy.wait_recv()
                for copy in forward(c - 1):
                    copy.start()
                for copy in to_mate(c - 1) + forward(c - 1):
                    copy.wait_recv()
                for copy in loads(c - 1):
                    copy.start()

            return carry

        lax.fori_loop(0, count + 2, turn, 0)

        def drain(c, carry):
            for copy in to_across(c) + to_mate(c) + forward(c):
                copy.wait_send()
            return carry

        lax.fori_loop(0, count, drain, 0)

        def out_copy(t):
            rows = pl.ds(pl.multiple_of(t * OUT_ROWS, OUT_ROWS), OUT_ROWS)
            slot = lax.rem(t, 2)
            return pltpu.make_async_copy(y_stage.at[slot], y_hbm.at[rows, :], y_sem.at[slot])

        def finish(t, carry):
            @pl.when(t >= 2)
            def _():
                out_copy(t - 2).wait()

            rows = pl.ds(pl.multiple_of(t * OUT_ROWS, OUT_ROWS), OUT_ROWS)
            y_stage[lax.rem(t, 2)] = (x_ref[rows, :].astype(jnp.float32) + total[rows, :]).astype(jnp.bfloat16)
            out_copy(t).start()
            return carry

        steps = tokens // OUT_ROWS
        lax.fori_loop(0, steps, finish, 0)
        for t in (steps - 2, steps - 1):
            out_copy(t).wait()


def stream_mlp(up_bf, down_bf, up_head, down_head, x):
    width, hidden = up_bf.shape
    tokens, model = x.shape
    count = hidden // CHUNK
    sems = pltpu.SemaphoreType.DMA((2, count))
    anywhere = pl.BlockSpec(memory_space=pl.ANY)
    bf16 = jnp.bfloat16
    return pl.pallas_call(
        stream_kernel,
        out_shape=(
            jax.ShapeDtypeStruct((tokens, model), bf16),
            jax.ShapeDtypeStruct((count, model, CHUNK), bf16),
            jax.ShapeDtypeStruct((count, CHUNK, model), bf16),
        ),
        in_specs=[anywhere] * 5,
        out_specs=(anywhere,) * 3,
        scratch_shapes=[
            pltpu.VMEM((tokens, model), bf16),
            pltpu.VMEM((tokens, model), jnp.float32),
            pltpu.VMEM((2, model, CHUNK), bf16),
            pltpu.VMEM((2, CHUNK, model), bf16),
            pltpu.VMEM((width, HEAD * CHUNK), bf16),
            pltpu.VMEM((HEAD * CHUNK, width), bf16),
            pltpu.VMEM((2, OUT_ROWS, model), bf16),
        ]
        + [sems] * 8
        + [
            pltpu.SemaphoreType.DMA((2, 2)),
            pltpu.SemaphoreType.DMA((2,)),
            pltpu.SemaphoreType.DMA,
            pltpu.SemaphoreType.DMA((2,)),
        ],
        compiler_params=pltpu.CompilerParams(
            collective_id=0, has_side_effects=True, vmem_limit_bytes=63 * 1024 * 1024
        ),
        cost_estimate=pl.CostEstimate(
            flops=4 * tokens * model * hidden, bytes_accessed=8 * model * hidden, transcendentals=tokens * hidden
        ),
    )(up_bf, down_bf, up_head, down_head, x)


def solution(mesh):
    up_spec = P("side", None, "rep", None)
    down_spec = P("side", None, None, "rep")
    act_spec = P("side", "rep", None)
    cross = [(r, r + mesh.shape["rep"]) for r in range(mesh.shape["rep"])]
    head = HEAD * CHUNK

    def device_step(w_up, w_down, g_up, g_down, learn_rate, prompts, prompt_lens):
        bf16 = jnp.bfloat16
        up_first = (w_up[0, 0, :, :head] - learn_rate * g_up[0, 0, :, :head]).astype(bf16)
        down_first = (w_down[0, 0, :head, :] - learn_rate * g_down[0, 0, :head, :]).astype(bf16)
        up_head = lax.ppermute(up_first, ("side", "rep"), cross)
        down_head = lax.ppermute(down_first, ("side", "rep"), cross)
        w_up, w_down, g_up, g_down, up_first, down_first = lax.optimization_barrier(
            (w_up, w_down, g_up, g_down, up_first, down_first)
        )
        new_up = w_up - learn_rate * g_up
        new_down = w_down - learn_rate * g_down
        y = stream_mlp(
            new_up[0, 0].astype(bf16), new_down[0, 0].astype(bf16), up_head, down_head, prompts[0]
        )[0]
        keep = (jnp.arange(y.shape[0])[:, None] < prompt_lens[0]) & (lax.axis_index("side") == 1)
        out = jnp.where(keep, y, jnp.zeros_like(y))
        return new_up, new_down, out[None]

    return jax.shard_map(
        device_step,
        mesh=mesh,
        in_specs=(up_spec, down_spec, up_spec, down_spec, P(), act_spec, P("rep")),
        out_specs=(up_spec, down_spec, act_spec),
        check_vma=False,
    )
```

time: 1040 us -> 685 us (0.66)
  waiting for transfers between devices: 707 us -> 0.01 us
  Pallas kernels: 0 us -> 606 us
  matrix products: 256 us -> 0 us
  other arithmetic: 52.2 us -> 71 us
  between operations: 15.4 us -> 2.01 us
    pallas_call x0 -> x1, Pallas kernels: none -> 606 us  [stream_mlp(): pl.pallas_call(stream_kernel, out_shape=(jax.ShapeDtypeStruct((tokens, mo...]
    ppermute x2, waiting for transfers between devices: 545 us -> 0.01 us  [the longest x1 0.01 us: device_step(): up_head = lax.ppermute(up_first, ('side', 'rep'), cross)]
    dot_general x2 -> x0, matrix products: 256 us -> none  [the longest x1 135 us: device_step(): jnp.dot(hidden, up_full[layer_idx], preferred_element_type=jnp.float32)]
    all_gather x2 -> x0, waiting for transfers between devices: 162 us -> none  [the longest x1 162 us: device_step(): down_full = lax.all_gather(down_sent, 'rep', axis=2, tiled=True)]
    broadcast_in_dim x0 -> x1, other arithmetic: none -> 10.9 us  [device_step(): return (new_up, new_down, out[None])]
    convert_element_type x2 -> x4, other arithmetic: 51.6 us -> 59.5 us  [the longest x1 30.6 us: device_step(): new_up[0, 0].astype(bf16)]
  transfers between devices with their start and end apart: 4 -> 2, of which waited for: 3 -> 0; matrix products, arithmetic and copies ran while one was open for 16% -> 8% of each run, Pallas kernels for 0% -> 0%
where the time goes in v1:
time: 685 us; the launch traced here: 684 us
  Pallas kernels  606 us (88%)
  other arithmetic  71 us (10%)
    pallas_call x1, Pallas kernels, stream_mlp(): pl.pallas_call(stream_kernel, out_shape=(jax.ShapeDtypeStruct((tokens, mo...  606 us
    convert_element_type x1, other arithmetic, device_step(): new_up[0, 0].astype(bf16)  30.6 us
    convert_element_type x1, other arithmetic, device_step(): new_down[0, 0].astype(bf16)  22.2 us
  transfers between devices with their start and end apart: 2, of which 0 were waited for; matrix products, arithmetic and copies ran while one was open for 8% of the time, Pallas kernels for 0%

profile of v1, /device:TPU:4, one launch (start us, length us, event | category | flops | bytes accessed | tf_op | source)
XLA Modules:
  0.0 684.0 jit_solution(9217928588550177635)
XLA Ops:
  1.3 2.7 fusion
  4.0 1.3 collective-permute-start
  5.3 0.0 slice-start
  5.3 3.9 fusion.1
  9.3 0.0 slice-start.1
  9.3 0.0 slice-start.2
  9.3 0.0 slice-start.3
  9.3 0.0 slice-start.4
  9.3 0.0 slice-start.5
  9.3 1.6 collective-permute-start.1
  10.8 30.6 %convert_bitcast_fusion.1 = (bf16[768,8192]{1,0:T(8,128)(2,1)}, f32[1,1,768,8192]{3,2,1,0:T(8,128)}) fusion(f32[1,1,768,8192]{3,2,1,0:T(8,128)} %param.7, f32[1,1,768,8192]{3,2,1,0:T(8,128)} %param.9, f32[]{:T(128)S(6)} %copy.10), kind=kLoop, calls=%fused_computation.4 | loop fusion | flops 18874368 | bytes 88080384 | tf_op jit(solution)/shard_map/convert_element_type | solution.py:258
  41.5 0.0 slice-done
  41.5 0.0 slice-done.1
  41.5 0.0 slice-done.2
  41.5 0.0 slice-done.3
  41.5 1.3 slice-done.4
  42.8 1.2 slice-done.5
  44.0 22.2 %convert_bitcast_fusion = (bf16[8192,768]{1,0:T(8,128)(2,1)}, f32[1,1,8192,768]{3,2,1,0:T(8,128)}) fusion(f32[1,1,8192,768]{3,2,1,0:T(8,128)S(1)} %bitcast.14, f32[1,1,8192,768]{3,2,1,0:T(8,128)} %param.10, f32[]{:T(128)S(6)} %copy.10), kind=kLoop, calls=%fused_computation.3 | loop fusion | flops 18874368 | bytes 88080384 | tf_op jit(solution)/shard_map/convert_element_type | solution.py:258
  66.9 0.6 fusion.2
  67.5 0.0 collective-permute-done.up_head
  67.5 0.0 collective-permute-done.1.down_head
  67.5 0.0 copy-start
  67.5 605.6 %shard_map.94 = (bf16[2048,3072]{1,0:T(8,128)(2,1)}, bf16[32,3072,256]{2,1,0:T(8,128)(2,1)}, bf16[32,256,3072]{2,1,0:T(8,128)(2,1)}) custom-call(bf16[768,8192]{1,0:T(8,128)(2,1)} %get-tuple-element.15.up_ref, bf16[8192,768]{1,0:T(8,128)(2,1)} %get-tuple-element.13.down_ref, bf16[768,768]{1,0:T(8,128)(2,1)} %collective-permute-done.up_head, ...), custom_call_target="tpu_custom_call" | custom-call | flops 206158430208 | bytes 201326592 | tf_op jit(solution)/shard_map/pallas_call | solution.py:205
  673.1 0.0 copy-done
  673.1 10.9 %select_bitcast_fusion = bf16[1,2048,3072]{2,1,0:T(8,128)(2,1)} fusion(bf16[2048,3072]{1,0:T(8,128)(2,1)} %get-tuple-element.12, pred[2048]{0:T(1024)(128)(4,1)S(1)} %copy-done), kind=kLoop, calls=%fused_computation.2 | loop fusion | flops 6291456 | bytes 25167872 | tf_op jit(solution)/shard_map/broadcast_in_dim | solution.py:262
  (1 shorter events, 0.0 us)
Async XLA Ops:
  4.0 63.4 %collective-permute-start = (bf16[768,768]{1,0:T(8,128)(2,1)S(1)}, bf16[768,768]{1,0:T(8,128)(2,1)}, u32[]{:S(2)}, u32[]{:S(2)}) collective-permute-start(bf16[768,768]{1,0:T(8,128)(2,1)S(1)} %fusion), channel_id=1, source_target_pairs={{0,4},{1,5},{2,6},{3,7}} | collective-permute-start | bytes 3538952 | tf_op jit(solution)/shard_map/ppermute | solution.py:250
  5.3 36.1 %slice-start = ((s8[25165824]{0:T(1024)(128)(4,1)}), s8[4194304]{0:T(1024)(128)(4,1)S(1)}, s32[]{:S(2)}) async-start(s8[25165824]{0:T(1024)(128)(4,1)} %bitcast.13), calls=%async_computation | async-start | bytes 8388608
  9.3 32.2 %slice-start.1 = ((s8[25165824]{0:T(1024)(128)(4,1)}), s8[4194304]{0:T(1024)(128)(4,1)S(1)}, s32[]{:S(2)}) async-start(s8[25165824]{0:T(1024)(128)(4,1)} %bitcast.13), calls=%async_computation.1 | async-start | bytes 8388608
  9.3 32.2 %slice-start.2 = ((s8[25165824]{0:T(1024)(128)(4,1)}), s8[4194304]{0:T(1024)(128)(4,1)S(1)}, s32[]{:S(2)}) async-start(s8[25165824]{0:T(1024)(128)(4,1)} %bitcast.13), calls=%async_computation.2 | async-start | bytes 8388608
  9.3 32.2 %slice-start.3 = ((s8[25165824]{0:T(1024)(128)(4,1)}), s8[4194304]{0:T(1024)(128)(4,1)S(1)}, s32[]{:S(2)}) async-start(s8[25165824]{0:T(1024)(128)(4,1)} %bitcast.13), calls=%async_computation.3 | async-start | bytes 8388608
  9.3 33.5 %slice-start.4 = ((s8[25165824]{0:T(1024)(128)(4,1)}), s8[4194304]{0:T(1024)(128)(4,1)S(1)}, s32[]{:S(2)}) async-start(s8[25165824]{0:T(1024)(128)(4,1)} %bitcast.13), calls=%async_computation.4 | async-start | bytes 8388608
  9.3 34.7 %slice-start.5 = ((s8[25165824]{0:T(1024)(128)(4,1)}), s8[4194304]{0:T(1024)(128)(4,1)S(1)}, s32[]{:S(2)}) async-start(s8[25165824]{0:T(1024)(128)(4,1)} %bitcast.13), calls=%async_computation.5 | async-start | bytes 8388608
  9.3 58.2 %collective-permute-start.1 = (bf16[768,768]{1,0:T(8,128)(2,1)}, bf16[768,768]{1,0:T(8,128)(2,1)}, u32[]{:S(2)}, u32[]{:S(2)}) collective-permute-start(bf16[768,768]{1,0:T(8,128)(2,1)} %fusion.1), channel_id=1, source_target_pairs={{0,4},{1,5},{2,6},{3,7}} | collective-permute-start | bytes 3538952 | tf_op jit(solution)/shard_map/ppermute | solution.py:251
  67.5 605.6 %copy-start = (pred[2048]{0:T(1024)(128)(4,1)S(1)}, pred[2048]{0:T(1024)(128)(4,1)}, u32[]{:S(2)}) copy-start(pred[2048]{0:T(1024)(128)(4,1)} %fusion.2) | copy-start | bytes 6148

commit v2 on v1

v2 whole, which is shorter than its diff:
```python
import jax
import jax.numpy as jnp
from jax import lax
from jax.experimental import pallas as pl
from jax.experimental.pallas import tpu as pltpu
from jax.sharding import PartitionSpec as P

MESH = pl.DeviceIdType.MESH
CHUNK = 256
HEAD = 1
ROWS = 512
COLS = 768
OUT_ROWS = 256
UP_TILE = 32
DOWN_TILE = 512
EARLY = 12
DEPTH = 3
STAGES = 4


def stream_kernel(
    up_w, up_g, down_w, down_g, rate_ref, up_head, down_head, x_hbm, order_ref,
    y_hbm, up_all, down_all,
    x_ref, total, up_slot, down_slot, up_bounce, down_bounce, y_stage,
    send_y, recv_y, send_x, recv_x, send_d, recv_d, send_f, recv_f,
    load_sem, fetch_sem, head_sem, x_sem, y_sem,
):
    side = lax.axis_index("side")
    me = lax.axis_index("rep")
    mate = me + 1 - 2 * lax.rem(me, 2)
    across = lax.rem(me + 2, 4)
    width = up_w.shape[0]
    count = up_w.shape[1] // CHUNK
    tokens = x_ref.shape[0]

    barrier = pltpu.get_barrier_semaphore()
    for peer in ((side, mate), (side, across), (1 - side, me)):
        pl.semaphore_signal(barrier, inc=1, device_id=peer, device_id_type=MESH)
    pl.semaphore_wait(barrier, 3)

    def wide(c):
        return pl.ds(pl.multiple_of(c * CHUNK, CHUNK), CHUNK)

    def piece(q):
        return pl.ds(pl.multiple_of(q * width, width), width)

    def remote(src, dst, send, recv, peer):
        return pltpu.make_async_remote_copy(
            src_ref=src, dst_ref=dst, send_sem=send, recv_sem=recv, device_id=peer, device_id_type=MESH
        )

    def down_link(c):
        stage = lax.rem(c, STAGES)
        up_part = up_slot.at[0, piece(stage), :]
        down_part = down_slot.at[0, :, piece(stage)]
        return (
            remote(up_part, up_all.at[c, piece(me), :], send_y.at[0, c], recv_y.at[0, c], (1, me)),
            remote(down_part, down_all.at[c, :, piece(me)], send_y.at[1, c], recv_y.at[1, c], (1, me)),
        )

    def relay(c, q, send, recv, peer):
        up_part = up_all.at[c, piece(q), :]
        down_part = down_all.at[c, :, piece(q)]
        return (
            remote(up_part, up_part, send.at[0, c], recv.at[0, c], (1, peer)),
            remote(down_part, down_part, send.at[1, c], recv.at[1, c], (1, peer)),
        )

    def to_across(c):
        return relay(c, me, send_x, recv_x, across)

    def to_mate(c):
        return relay(c, me, send_d, recv_d, mate)

    def forward(c):
        return relay(c, across, send_f, recv_f, mate)

    def loads(c):
        slot = lax.rem(c, 2)
        return (
            pltpu.make_async_copy(up_all.at[c], up_slot.at[slot], load_sem.at[0, slot]),
            pltpu.make_async_copy(down_all.at[c], down_slot.at[slot], load_sem.at[1, slot]),
        )

    @pl.when(side == 0)
    def _():
        rate = rate_ref[0]

        def up_view(slot, k):
            return total.at[pl.ds(0, width), pl.ds(pl.multiple_of((2 * slot + k) * CHUNK, CHUNK), CHUNK)]

        def down_view(slot, k):
            return total.at[pl.ds(pl.multiple_of(width + (2 * slot + k) * CHUNK, CHUNK), CHUNK), pl.ds(0, width)]

        def fetches(c):
            slot = lax.rem(c, 2)
            return (
                pltpu.make_async_copy(up_w.at[:, wide(c)], up_view(slot, 0), fetch_sem.at[slot, 0]),
                pltpu.make_async_copy(up_g.at[:, wide(c)], up_view(slot, 1), fetch_sem.at[slot, 1]),
                pltpu.make_async_copy(down_w.at[wide(c), :], down_view(slot, 0), fetch_sem.at[slot, 2]),
                pltpu.make_async_copy(down_g.at[wide(c), :], down_view(slot, 1), fetch_sem.at[slot, 3]),
            )

        for c in (HEAD, HEAD + 1):
            for copy in fetches(c):
                copy.start()

        def send(c, carry):
            @pl.when(c < count)
            def _():
                slot = lax.rem(c, 2)
                stage = lax.rem(c, STAGES)
                for copy in fetches(c):
                    copy.wait()

                @pl.when(c >= HEAD + STAGES)
                def _():
                    for copy in down_link(c - STAGES):
                        copy.wait_send()

                up_slot[0, piece(stage), :] = (up_view(slot, 0)[...] - rate * up_view(slot, 1)[...]).astype(jnp.bfloat16)
                down_slot[0, :, piece(stage)] = (
                    down_view(slot, 0)[...] - rate * down_view(slot, 1)[...]
                ).astype(jnp.bfloat16)

                @pl.when(c + 2 < count)
                def _():
                    for copy in fetches(c + 2):
                        copy.start()

            @pl.when(c > HEAD)
            def _():
                for copy in down_link(c - 1):
                    copy.start()

            return carry

        lax.fori_loop(HEAD, count + 1, send, 0)
        for c in range(count - STAGES, count):
            for copy in down_link(c):
                copy.wait_send()

    @pl.when(side == 1)
    def _():
        x_copy = pltpu.make_async_copy(x_hbm, x_ref, x_sem)
        heads = (
            pltpu.make_async_copy(up_head, up_bounce, head_sem.at[0]),
            pltpu.make_async_copy(down_head, down_bounce, head_sem.at[1]),
        )
        for copy in heads:
            copy.start()
        for copy in heads:
            copy.wait()
        x_copy.start()
        places = []
        for c in range(HEAD):
            part = slice(c * CHUNK, (c + 1) * CHUNK)
            places.append(
                pltpu.make_async_copy(up_bounce.at[:, part], up_all.at[c, piece(me), :], send_y.at[0, c])
            )
            places.append(
                pltpu.make_async_copy(down_bounce.at[part, :], down_all.at[c, :, piece(me)], send_y.at[1, c])
            )
        for copy in places:
            copy.start()
        for copy in places:
            copy.wait()

        def fetch(c):
            for copy in to_mate(c) + forward(c):
                copy.wait_recv()
            for copy in loads(c):
                copy.start()

        def compute(c):
            slot = lax.rem(c, 2)

            def block(t, carry):
                rows = pl.ds(pl.multiple_of(t * ROWS, ROWS), ROWS)
                pre = jnp.dot(x_ref[rows, :], up_slot[slot], preferred_element_type=jnp.float32)
                act = jax.nn.gelu(pre, approximate=True).astype(jnp.bfloat16)
                for n in range(0, total.shape[1], COLS):
                    total[rows, n : n + COLS] += jnp.dot(
                        act, down_slot[slot, :, n : n + COLS], preferred_element_type=jnp.float32
                    )

                @pl.when((t == 1) & (c + 1 < count))
                def _():
                    fetch(c + 1)

                return carry

            lax.fori_loop(0, tokens // ROWS, block, 0)

        def turn(c, carry):
            @pl.when(c < count)
            def _():
                @pl.when(c >= HEAD)
                def _():
                    for copy in down_link(c):
                        copy.wait_recv()

                for copy in to_across(c) + to_mate(c):
                    copy.start()

            @pl.when(c == 0)
            def _():
                total[...] = jnp.zeros_like(total)

            @pl.when((c >= 1) & (c <= count))
            def _():
                for copy in to_across(c - 1):
                    copy.wait_recv()
                for copy in forward(c - 1):
                    copy.start()

            @pl.when(c == 1)
            def _():
                fetch(0)
                x_copy.wait()

            @pl.when(c >= 2)
            def _():
                for copy in loads(c - 2):
                    copy.wait()
                compute(c - 2)

            return carry

        lax.fori_loop(0, count + 2, turn, 0)

        def out_copy(t):
            rows = pl.ds(pl.multiple_of(t * OUT_ROWS, OUT_ROWS), OUT_ROWS)
            slot = lax.rem(t, 2)
            return pltpu.make_async_copy(y_stage.at[slot], y_hbm.at[rows, :], y_sem.at[slot])

        def finish(t, carry):
            @pl.when(t >= 2)
            def _():
                out_copy(t - 2).wait()

            rows = pl.ds(pl.multiple_of(t * OUT_ROWS, OUT_ROWS), OUT_ROWS)
            y_stage[lax.rem(t, 2)] = (x_ref[rows, :].astype(jnp.float32) + total[rows, :]).astype(jnp.bfloat16)
            out_copy(t).start()
            return carry

        steps = tokens // OUT_ROWS
        lax.fori_loop(0, steps, finish, 0)

        def drain(c, carry):
            for copy in to_across(c) + to_mate(c) + forward(c):
                copy.wait_send()
            return carry

        lax.fori_loop(0, count, drain, 0)
        for t in (steps - 2, steps - 1):
            out_copy(t).wait()


def sweep(first, last, ins, outs, work):
    for i in (first, first + 1):
        for copy in ins(i):
            copy.start()

    def step(i, carry):
        @pl.when(i + 2 < last)
        def _():
            for copy in ins(i + 2):
                copy.start()

        for copy in ins(i):
            copy.wait()

        @pl.when(i >= first + DEPTH)
        def _():
            for copy in outs(i - DEPTH):
                copy.wait()

        work(lax.rem(i, DEPTH), i)
        for copy in outs(i):
            copy.start()
        return carry

    lax.fori_loop(first, last, step, 0)
    for i in range(last - DEPTH, last):
        for copy in outs(i):
            copy.wait()


def update_rows(first, last, tile, w, g, new, rate, w_buf, g_buf, n_buf, sems):
    def rows(i):
        return pl.ds(pl.multiple_of(i * tile, tile), tile)

    def ins(i):
        slot = lax.rem(i, DEPTH)
        return (
            pltpu.make_async_copy(w.at[rows(i), :], w_buf.at[slot], sems.at[0, slot]),
            pltpu.make_async_copy(g.at[rows(i), :], g_buf.at[slot], sems.at[1, slot]),
        )

    def outs(i):
        slot = lax.rem(i, DEPTH)
        return (pltpu.make_async_copy(n_buf.at[slot], new.at[rows(i), :], sems.at[2, slot]),)

    def work(slot, i):
        n_buf[slot] = w_buf[slot] - rate * g_buf[slot]

    sweep(first, last, ins, outs, work)


def early_kernel(up_w, up_g, rate_ref, up_new, down_new, w_buf, g_buf, n_buf, zero_down, sems, zero_sem):
    side = lax.axis_index("side")

    @pl.when(side == 0)
    def _():
        update_rows(0, EARLY, UP_TILE, up_w, up_g, up_new, rate_ref[0], w_buf, g_buf, n_buf, sems)

    @pl.when(side == 1)
    def _():
        n_buf[0] = jnp.zeros_like(n_buf[0])
        zero_down[...] = jnp.zeros_like(zero_down)
        copies = []
        for i in range(up_new.shape[0] // UP_TILE):
            copies.append(pltpu.make_async_copy(n_buf.at[0], up_new.at[pl.ds(i * UP_TILE, UP_TILE), :], zero_sem))
        for i in range(down_new.shape[0] // DOWN_TILE):
            copies.append(pltpu.make_async_copy(zero_down, down_new.at[pl.ds(i * DOWN_TILE, DOWN_TILE), :], zero_sem))
        for copy in copies:
            copy.start()
        for copy in copies:
            copy.wait()


def late_kernel(
    up_w, up_g, down_w, down_g, rate_ref, len_ref, y, up_in, down_in,
    up_new, down_new, out,
    w_buf, g_buf, n_buf, dw_buf, dg_buf, dn_buf, y_buf, o_buf, sems, d_sems, y_sems,
):
    side = lax.axis_index("side")
    steps = out.shape[0] // OUT_ROWS

    def rows(i):
        return pl.ds(pl.multiple_of(i * OUT_ROWS, OUT_ROWS), OUT_ROWS)

    @pl.when(side == 0)
    def _():
        rate = rate_ref[0]
        o_buf[0] = jnp.zeros_like(o_buf[0])
        zeros = [
            pltpu.make_async_copy(o_buf.at[0], out.at[pl.ds(i * OUT_ROWS, OUT_ROWS), :], y_sems.at[1, 0])
            for i in range(steps)
        ]
        for copy in zeros:
            copy.start()
        tiles = up_new.shape[0] // UP_TILE
        update_rows(EARLY, tiles, UP_TILE, up_w, up_g, up_new, rate, w_buf, g_buf, n_buf, sems)
        tiles = down_new.shape[0] // DOWN_TILE
        update_rows(0, tiles, DOWN_TILE, down_w, down_g, down_new, rate, dw_buf, dg_buf, dn_buf, d_sems)
        for copy in zeros:
            copy.wait()

    @pl.when(side == 1)
    def _():
        def ins(i):
            slot = lax.rem(i, DEPTH)
            return (pltpu.make_async_copy(y.at[rows(i), :], y_buf.at[slot], y_sems.at[0, slot]),)

        def outs(i):
            slot = lax.rem(i, DEPTH)
            return (pltpu.make_async_copy(o_buf.at[slot], out.at[rows(i), :], y_sems.at[1, slot]),)

        def work(slot, i):
            row = i * OUT_ROWS + lax.broadcasted_iota(jnp.int32, (OUT_ROWS, out.shape[1]), 0)
            tile = y_buf[slot]
            o_buf[slot] = jnp.where(row < len_ref[0], tile, jnp.zeros_like(tile))

        sweep(0, steps, ins, outs, work)


ANY = pl.BlockSpec(memory_space=pl.ANY)
SMEM = pl.BlockSpec(memory_space=pltpu.SMEM)
DMA = pltpu.SemaphoreType.DMA
F32 = jnp.float32
BF16 = jnp.bfloat16


def early(up_w, up_g, rate, down_shape):
    hidden = up_w.shape[1]
    band = pltpu.VMEM((DEPTH, UP_TILE, hidden), F32)
    return pl.pallas_call(
        early_kernel,
        out_shape=(jax.ShapeDtypeStruct(up_w.shape, F32), jax.ShapeDtypeStruct(down_shape, F32)),
        in_specs=[ANY, ANY, SMEM],
        out_specs=(ANY, ANY),
        scratch_shapes=[band] * 3 + [pltpu.VMEM((DOWN_TILE, down_shape[1]), F32), DMA((3, DEPTH)), DMA],
        compiler_params=pltpu.CompilerParams(vmem_limit_bytes=63 * 1024 * 1024),
        cost_estimate=pl.CostEstimate(flops=40_000_000, bytes_accessed=50_000_000, transcendentals=0),
    )(up_w, up_g, rate)


def late(up_w, up_g, down_w, down_g, rate, lens, y, up_new, down_new):
    hidden, width = down_w.shape
    up_band = pltpu.VMEM((DEPTH, UP_TILE, hidden), F32)
    down_band = pltpu.VMEM((DEPTH, DOWN_TILE, width), F32)
    row_band = pltpu.VMEM((DEPTH, OUT_ROWS, y.shape[1]), BF16)
    return pl.pallas_call(
        late_kernel,
        out_shape=(
            jax.ShapeDtypeStruct(up_w.shape, F32),
            jax.ShapeDtypeStruct(down_w.shape, F32),
            jax.ShapeDtypeStruct(y.shape, BF16),
        ),
        in_specs=[ANY] * 4 + [SMEM, SMEM] + [ANY] * 3,
        out_specs=(ANY,) * 3,
        scratch_shapes=[up_band] * 3 + [down_band] * 3 + [row_band] * 2
        + [DMA((3, DEPTH)), DMA((3, DEPTH)), DMA((2, DEPTH))],
        input_output_aliases={7: 0, 8: 1},
        compiler_params=pltpu.CompilerParams(vmem_limit_bytes=63 * 1024 * 1024),
        cost_estimate=pl.CostEstimate(flops=40_000_000, bytes_accessed=100_000_000, transcendentals=0),
    )(up_w, up_g, down_w, down_g, rate, lens, y, up_new, down_new)


def stream_mlp(up_w, up_g, down_w, down_g, rate, up_head, down_head, x, order):
    width, hidden = up_w.shape
    tokens, model = x.shape
    count = hidden // CHUNK
    return pl.pallas_call(
        stream_kernel,
        out_shape=(
            jax.ShapeDtypeStruct((tokens, model), BF16),
            jax.ShapeDtypeStruct((count, model, CHUNK), BF16),
            jax.ShapeDtypeStruct((count, CHUNK, model), BF16),
        ),
        in_specs=[ANY] * 4 + [SMEM] + [ANY] * 4,
        out_specs=(ANY,) * 3,
        scratch_shapes=[
            pltpu.VMEM((tokens, model), BF16),
            pltpu.VMEM((tokens, model), F32),
            pltpu.VMEM((2, model, CHUNK), BF16),
            pltpu.VMEM((2, CHUNK, model), BF16),
            pltpu.VMEM((width, HEAD * CHUNK), BF16),
            pltpu.VMEM((HEAD * CHUNK, width), BF16),
            pltpu.VMEM((2, OUT_ROWS, model), BF16),
        ]
        + [DMA((2, count))] * 8
        + [DMA((2, 2)), DMA((2, 4)), DMA((2,)), DMA, DMA((2,))],
        compiler_params=pltpu.CompilerParams(
            collective_id=0, has_side_effects=True, vmem_limit_bytes=63 * 1024 * 1024
        ),
        cost_estimate=pl.CostEstimate(
            flops=4 * tokens * model * hidden, bytes_accessed=8 * model * hidden, transcendentals=tokens * hidden
        ),
    )(up_w, up_g, down_w, down_g, rate, up_head, down_head, x, order)


def solution(mesh):
    up_spec = P("side", None, "rep", None)
    down_spec = P("side", None, None, "rep")
    act_spec = P("side", "rep", None)
    cross = [(r, r + mesh.shape["rep"]) for r in range(mesh.shape["rep"])]
    head = HEAD * CHUNK

    def device_step(w_up, w_down, g_up, g_down, learn_rate, prompts, prompt_lens):
        up_w, up_g, down_w, down_g = w_up[0, 0], g_up[0, 0], w_down[0, 0], g_down[0, 0]
        up_first = (up_w[:, :head] - learn_rate * up_g[:, :head]).astype(BF16)
        down_first = (down_w[:head, :] - learn_rate * down_g[:head, :]).astype(BF16)
        up_head = lax.ppermute(up_first, ("side", "rep"), cross)
        down_head = lax.ppermute(down_first, ("side", "rep"), cross)
        rate = learn_rate.reshape(1)
        up_part, down_part = early(up_w, up_g, rate, down_w.shape)
        y = stream_mlp(up_w, up_g, down_w, down_g, rate, up_head, down_head, prompts[0], down_part)[0]
        new_up, new_down, out = late(up_w, up_g, down_w, down_g, rate, prompt_lens, y, up_part, down_part)
        return new_up[None, None], new_down[None, None], out[None]

    return jax.shard_map(
        device_step,
        mesh=mesh,
        in_specs=(up_spec, down_spec, up_spec, down_spec, P(), act_spec, P("rep")),
        out_specs=(up_spec, down_spec, act_spec),
        check_vma=False,
    )
```

time: 685 us -> 619 us (0.904)
  other arithmetic: 71 us -> 2.98 us
    convert_element_type x4 -> x2, other arithmetic: 59.5 us -> 2.98 us  [the longest x1 1.5 us: device_step(): up_first = (up_w[:, :head] - learn_rate * up_g[:, :head]).astype(BF16)]
    pallas_call x0 -> x2, Pallas kernels: none -> 25.9 us  [the longest x1 16.1 us: early(): pl.pallas_call(early_kernel, out_shape=(jax.ShapeDtypeStruct(up_w.shape,...]
    pallas_call x1, Pallas kernels: 606 us -> 585 us  [stream_mlp(): pl.pallas_call(stream_kernel, out_shape=(jax.ShapeDtypeStruct((tokens, mo...]
    broadcast_in_dim x1 -> x0, other arithmetic: 10.9 us -> none  [device_step(): return (new_up, new_down, out[None])]
  transfers between devices with their start and end apart: 2 -> 2, of which waited for: 0 -> 1; matrix products, arithmetic and copies ran while one was open for 8% -> 0% of each run, Pallas kernels for 0% -> 3%
where the time goes in v2:
time: 619 us
  Pallas kernels  611 us (99%)
    pallas_call x1, Pallas kernels, stream_mlp(): pl.pallas_call(stream_kernel, out_shape=(jax.ShapeDtypeStruct((tokens, mo...  585 us
    pallas_call x1, Pallas kernels, early(): pl.pallas_call(early_kernel, out_shape=(jax.ShapeDtypeStruct(up_w.shape,...  16.1 us
  transfers between devices with their start and end apart: 2, of which 1 were waited for; matrix products, arithmetic and copies ran while one was open for 0% of the time, Pallas kernels for 3%

profile of v2, /device:TPU:4, one launch (start us, length us, event | category | flops | bytes accessed | tf_op | source)
XLA Modules:
  0.0 618.7 jit_solution(10883301469904737637)
XLA Ops:
  1.3 1.5 fusion.1
  2.8 1.3 collective-permute-start
  4.1 1.5 fusion.2
  5.6 1.3 collective-permute-start.1
  7.5 16.1 %shard_map.94 = (f32[768,8192]{1,0:T(8,128)}, f32[8192,768]{1,0:T(8,128)}) custom-call(f32[768,8192]{1,0:T(8,128)} %bitcast.15, f32[768,8192]{1,0:T(8,128)} %bitcast.19, f32[1]{0:T(128)} %bitcast.11.rate_ref), custom_call_target="tpu_custom_call" | custom-call | flops 40000000 | bytes 50000000 | tf_op jit(solution)/shard_map/pallas_call | solution.py:389
  23.6 0.0 collective-permute-done.up_head
  23.6 0.3 collective-permute-done.1.down_head
  24.0 584.9 %shard_map.95 = (bf16[2048,3072]{1,0:T(8,128)(2,1)}, bf16[32,3072,256]{2,1,0:T(8,128)(2,1)}, bf16[32,256,3072]{2,1,0:T(8,128)(2,1)}) custom-call(f32[768,8192]{1,0:T(8,128)} %bitcast.16, f32[768,8192]{1,0:T(8,128)} %bitcast.20, f32[8192,768]{1,0:T(8,128)} %bitcast.22, f32[8192,768]{1,0:T(8,128)} %bitcast.24, f32[1]{0:T(128)} %bitcast.12.rate_ref, ...), custom_call_target="tpu_custom_call" | custom-call | flops 206158430208 | bytes 201326592 | tf_op jit(solution)/shard_map/pallas_call | solution.py:426
  608.9 9.8 %shard_map.96 = (f32[768,8192]{1,0:T(8,128)}, f32[8192,768]{1,0:T(8,128)}, bf16[2048,3072]{1,0:T(8,128)(2,1)}) custom-call(f32[768,8192]{1,0:T(8,128)} %bitcast.17, f32[768,8192]{1,0:T(8,128)} %bitcast.21, f32[8192,768]{1,0:T(8,128)} %bitcast.23, f32[8192,768]{1,0:T(8,128)} %bitcast.25, ...), custom_call_target="tpu_custom_call", output_to_operand_aliasing={{0}: (7, {}), {1}: (8, {})} | custom-call | flops 40000000 | bytes 100000000 | tf_op jit(solution)/shard_map/pallas_call | solution.py:405
Async XLA Ops:
  2.8 20.8 %collective-permute-start = (bf16[768,256]{1,0:T(8,128)(2,1)S(1)}, bf16[768,256]{1,0:T(8,128)(2,1)}, u32[]{:S(2)}, u32[]{:S(2)}) collective-permute-start(bf16[768,256]{1,0:T(8,128)(2,1)S(1)} %fusion.1), channel_id=1, source_target_pairs={{0,4},{1,5},{2,6},{3,7}} | collective-permute-start | bytes 1179656 | tf_op jit(solution)/shard_map/ppermute | solution.py:466
  5.6 18.4 %collective-permute-start.1 = (bf16[256,768]{1,0:T(8,128)(2,1)S(1)}, bf16[256,768]{1,0:T(8,128)(2,1)}, u32[]{:S(2)}, u32[]{:S(2)}) collective-permute-start(bf16[256,768]{1,0:T(8,128)(2,1)S(1)} %fusion.2), channel_id=1, source_target_pairs={{0,4},{1,5},{2,6},{3,7}} | collective-permute-start | bytes 1179656 | tf_op jit(solution)/shard_map/ppermute | solution.py:467

commit v3 on v2

--- a/solution.py
+++ b/solution.py
@@ -13,7 +13,9 @@
 OUT_ROWS = 256
 UP_TILE = 32
 DOWN_TILE = 512
-EARLY = 12
+EARLY = 14
+OUT_SLOTS = ROWS // OUT_ROWS
+LAG = 4
 DEPTH = 3
 STAGES = 4
 
@@ -33,10 +35,11 @@
     count = up_w.shape[1] // CHUNK
     tokens = x_ref.shape[0]
 
-    barrier = pltpu.get_barrier_semaphore()
-    for peer in ((side, mate), (side, across), (1 - side, me)):
-        pl.semaphore_signal(barrier, inc=1, device_id=peer, device_id_type=MESH)
-    pl.semaphore_wait(barrier, 3)
+    def meet():
+        barrier = pltpu.get_barrier_semaphore()
+        for peer in ((side, mate), (side, across), (1 - side, me)):
+            pl.semaphore_signal(barrier, inc=1, device_id=peer, device_id_type=MESH)
+        pl.semaphore_wait(barrier, 3)
 
     def wide(c):
         return pl.ds(pl.multiple_of(c * CHUNK, CHUNK), CHUNK)
@@ -104,14 +107,23 @@
         for c in (HEAD, HEAD + 1):
             for copy in fetches(c):
                 copy.start()
+        meet()
 
         def send(c, carry):
             @pl.when(c < count)
             def _():
+                for copy in fetches(c):
+                    copy.wait()
+
+            @pl.when(c > HEAD)
+            def _():
+                for copy in down_link(c - 1):
+                    copy.start()
+
+            @pl.when(c < count)
+            def _():
                 slot = lax.rem(c, 2)
                 stage = lax.rem(c, STAGES)
-                for copy in fetches(c):
-                    copy.wait()
 
                 @pl.when(c >= HEAD + STAGES)
                 def _():
@@ -128,11 +140,6 @@
                     for copy in fetches(c + 2):
                         copy.start()
 
-            @pl.when(c > HEAD)
-            def _():
-                for copy in down_link(c - 1):
-                    copy.start()
-
             return carry
 
         lax.fori_loop(HEAD, count + 1, send, 0)
@@ -149,112 +156,117 @@
         )
         for copy in heads:
             copy.start()
+        meet()
+        for peer, send, recv in ((across, send_x, recv_x), (mate, send_d, recv_d)):
+            remote(up_head, up_all.at[0, piece(me), :], send.at[0, 0], recv.at[0, 0], (1, peer)).start()
+            remote(down_head, down_all.at[0, :, piece(me)], send.at[1, 0], recv.at[1, 0], (1, peer)).start()
         for copy in heads:
             copy.wait()
+        places = (
+            pltpu.make_async_copy(up_bounce, up_all.at[0, piece(me), :], head_sem.at[0]),
+            pltpu.make_async_copy(down_bounce, down_all.at[0, :, piece(me)], head_sem.at[1]),
+        )
+        for copy in places:
+            copy.start()
         x_copy.start()
-        places = []
-        for c in range(HEAD):
-            part = slice(c * CHUNK, (c + 1) * CHUNK)
-            places.append(
-                pltpu.make_async_copy(up_bounce.at[:, part], up_all.at[c, piece(me), :], send_y.at[0, c])
-            )
-            places.append(
-                pltpu.make_async_copy(down_bounce.at[part, :], down_all.at[c, :, piece(me)], send_y.at[1, c])
-            )
+        total[...] = jnp.zeros_like(total)
         for copy in places:
-            copy.start()
-        for copy in places:
-            copy.wait()
-
-        def fetch(c):
-            for copy in to_mate(c) + forward(c):
+            copy.wait()
+        x_copy.wait()
+
+        def pass_on(c, half):
+            down_link(c)[half].wait_recv()
+            to_across(c)[half].start()
+            to_mate(c)[half].start()
+
+        def spread(c):
+            for copy in to_across(c):
                 copy.wait_recv()
-            for copy in loads(c):
+            for copy in forward(c):
                 copy.start()
 
-        def compute(c):
+        def settle(c):
+            for copy in to_across(c) + to_mate(c) + forward(c):
+                copy.wait_send()
+
+        def out_copy(t):
+            rows = pl.ds(pl.multiple_of(t * OUT_ROWS, OUT_ROWS), OUT_ROWS)
+            slot = lax.rem(t, OUT_SLOTS)
+            return pltpu.make_async_copy(y_stage.at[slot], y_hbm.at[rows, :], y_sem.at[slot])
+
+        def block(c, t):
             slot = lax.rem(c, 2)
-
-            def block(t, carry):
-                rows = pl.ds(pl.multiple_of(t * ROWS, ROWS), ROWS)
-                pre = jnp.dot(x_ref[rows, :], up_slot[slot], preferred_element_type=jnp.float32)
-                act = jax.nn.gelu(pre, approximate=True).astype(jnp.bfloat16)
-                for n in range(0, total.shape[1], COLS):
-                    total[rows, n : n + COLS] += jnp.dot(
-                        act, down_slot[slot, :, n : n + COLS], preferred_element_type=jnp.float32
-                    )
-
-                @pl.when((t == 1) & (c + 1 < count))
-                def _():
-                    fetch(c + 1)
-
-                return carry
-
-            lax.fori_loop(0, tokens // ROWS, block, 0)
+            rows = pl.ds(pl.multiple_of(t * ROWS, ROWS), ROWS)
+            pre = jnp.dot(x_ref[rows, :], up_slot[slot], preferred_element_type=jnp.float32)
+            act = jax.nn.gelu(pre, approximate=True).astype(jnp.bfloat16)
+            for n in range(0, total.shape[1], COLS):
+                total[rows, n : n + COLS] += jnp.dot(
+                    act, down_slot[slot, :, n : n + COLS], preferred_element_type=jnp.float32
+                )
+
+            @pl.when(c == count - 1)
+            def _():
+                for j in range(OUT_SLOTS):
+                    k = t * OUT_SLOTS + j
+
+                    @pl.when(t > 0)
+                    def _():
+                        out_copy(k - OUT_SLOTS).wait()
+
+                    part = pl.ds(pl.multiple_of(k * OUT_ROWS, OUT_ROWS), OUT_ROWS)
+                    y_stage[j] = (x_ref[part, :].astype(jnp.float32) + total[part, :]).astype(jnp.bfloat16)
+                    out_copy(k).start()
+
+        last = tokens // ROWS - 1
+        pass_on(1, 0)
+        spread(0)
 
         def turn(c, carry):
             @pl.when(c < count)
             def _():
-                @pl.when(c >= HEAD)
-                def _():
-                    for copy in down_link(c):
-                        copy.wait_recv()
-
-                for copy in to_across(c) + to_mate(c):
+                pass_on(c, 1)
+
+            @pl.when(c <= count)
+            def _():
+                for copy in to_mate(c - 1) + forward(c - 1):
+                    copy.wait_recv()
+                for copy in loads(c - 1):
                     copy.start()
 
-            @pl.when(c == 0)
-            def _():
-                total[...] = jnp.zeros_like(total)
-
-            @pl.when((c >= 1) & (c <= count))
-            def _():
-                for copy in to_across(c - 1):
-                    copy.wait_recv()
-                for copy in forward(c - 1):
-                    copy.start()
-
-            @pl.when(c == 1)
-            def _():
-                fetch(0)
-                x_copy.wait()
-
             @pl.when(c >= 2)
             def _():
-                for copy in loads(c - 2):
+                block(c - 2, last)
+
+            @pl.when(c <= count)
+            def _():
+                for copy in loads(c - 1):
                     copy.wait()
-                compute(c - 2)
+
+                def part(t, carry):
+                    block(c - 1, t)
+                    return carry
+
+                lax.fori_loop(0, last, part, 0)
+
+            @pl.when(c + 1 < count)
+            def _():
+                pass_on(c + 1, 0)
+
+            @pl.when(c < count)
+            def _():
+                spread(c)
+
+            @pl.when(c >= LAG)
+            def _():
+                settle(c - LAG)
 
             return carry
 
-        lax.fori_loop(0, count + 2, turn, 0)
-
-        def out_copy(t):
-            rows = pl.ds(pl.multiple_of(t * OUT_ROWS, OUT_ROWS), OUT_ROWS)
-            slot = lax.rem(t, 2)
-            return pltpu.make_async_copy(y_stage.at[slot], y_hbm.at[rows, :], y_sem.at[slot])
-
-        def finish(t, carry):
-            @pl.when(t >= 2)
-            def _():
-                out_copy(t - 2).wait()
-
-            rows = pl.ds(pl.multiple_of(t * OUT_ROWS, OUT_ROWS), OUT_ROWS)
-            y_stage[lax.rem(t, 2)] = (x_ref[rows, :].astype(jnp.float32) + total[rows, :]).astype(jnp.bfloat16)
-            out_copy(t).start()
-            return carry
-
-        steps = tokens // OUT_ROWS
-        lax.fori_loop(0, steps, finish, 0)
-
-        def drain(c, carry):
-            for copy in to_across(c) + to_mate(c) + forward(c):
-                copy.wait_send()
-            return carry
-
-        lax.fori_loop(0, count, drain, 0)
-        for t in (steps - 2, steps - 1):
-            out_copy(t).wait()
+        lax.fori_loop(1, count + 2, turn, 0)
+        for c in range(count + 2 - LAG, count):
+            settle(c)
+        for k in range((last + 1) * OUT_SLOTS - OUT_SLOTS, (last + 1) * OUT_SLOTS):
+            out_copy(k).wait()
 
 
 def sweep(first, last, ins, outs, work):
@@ -439,7 +451,7 @@
             pltpu.VMEM((2, CHUNK, model), BF16),
             pltpu.VMEM((width, HEAD * CHUNK), BF16),
             pltpu.VMEM((HEAD * CHUNK, width), BF16),
-            pltpu.VMEM((2, OUT_ROWS, model), BF16),
+            pltpu.VMEM((OUT_SLOTS, OUT_ROWS, model), BF16),
         ]
         + [DMA((2, count))] * 8
         + [DMA((2, 2)), DMA((2, 4)), DMA((2,)), DMA, DMA((2,))],

time: 619 us -> 621 us (level)
  no operation moved by 1% of the time
where the time goes in v3:
time: 621 us; the launch traced here: 620 us
  Pallas kernels  612 us (99%)
    pallas_call x1, Pallas kernels, stream_mlp(): pl.pallas_call(stream_kernel, out_shape=(jax.ShapeDtypeStruct((tokens, mo...  586 us
    pallas_call x1, Pallas kernels, early(): pl.pallas_call(early_kernel, out_shape=(jax.ShapeDtypeStruct(up_w.shape,...  16.1 us
  transfers between devices with their start and end apart: 2, of which 1 were waited for; matrix products, arithmetic and copies ran while one was open for 0% of the time, Pallas kernels for 3%

profile of v3, /device:TPU:4, one launch (start us, length us, event | category | flops | bytes accessed | tf_op | source)
XLA Modules:
  0.0 619.9 jit_solution(13410049471267919271)
XLA Ops:
  1.3 1.5 fusion.1
  2.8 1.3 collective-permute-start
  4.1 1.5 fusion.2
  5.6 1.3 collective-permute-start.1
  7.5 16.1 %shard_map.94 = (f32[768,8192]{1,0:T(8,128)}, f32[8192,768]{1,0:T(8,128)}) custom-call(f32[768,8192]{1,0:T(8,128)} %bitcast.15, f32[768,8192]{1,0:T(8,128)} %bitcast.19, f32[1]{0:T(128)} %bitcast.11.rate_ref), custom_call_target="tpu_custom_call" | custom-call | flops 40000000 | bytes 50000000 | tf_op jit(solution)/shard_map/pallas_call | solution.py:401
  23.6 0.0 collective-permute-done.up_head
  23.6 0.3 collective-permute-done.1.down_head
  24.0 586.1 %shard_map.95 = (bf16[2048,3072]{1,0:T(8,128)(2,1)}, bf16[32,3072,256]{2,1,0:T(8,128)(2,1)}, bf16[32,256,3072]{2,1,0:T(8,128)(2,1)}) custom-call(f32[768,8192]{1,0:T(8,128)} %bitcast.16, f32[768,8192]{1,0:T(8,128)} %bitcast.20, f32[8192,768]{1,0:T(8,128)} %bitcast.22, f32[8192,768]{1,0:T(8,128)} %bitcast.24, f32[1]{0:T(128)} %bitcast.12.rate_ref, ...), custom_call_target="tpu_custom_call" | custom-call | flops 206158430208 | bytes 201326592 | tf_op jit(solution)/shard_map/pallas_call | solution.py:438
  610.1 9.8 %shard_map.96 = (f32[768,8192]{1,0:T(8,128)}, f32[8192,768]{1,0:T(8,128)}, bf16[2048,3072]{1,0:T(8,128)(2,1)}) custom-call(f32[768,8192]{1,0:T(8,128)} %bitcast.17, f32[768,8192]{1,0:T(8,128)} %bitcast.21, f32[8192,768]{1,0:T(8,128)} %bitcast.23, f32[8192,768]{1,0:T(8,128)} %bitcast.25, ...), custom_call_target="tpu_custom_call", output_to_operand_aliasing={{0}: (7, {}), {1}: (8, {})} | custom-call | flops 40000000 | bytes 100000000 | tf_op jit(solution)/shard_map/pallas_call | solution.py:417
Async XLA Ops:
  2.8 20.8 %collective-permute-start = (bf16[768,256]{1,0:T(8,128)(2,1)S(1)}, bf16[768,256]{1,0:T(8,128)(2,1)}, u32[]{:S(2)}, u32[]{:S(2)}) collective-permute-start(bf16[768,256]{1,0:T(8,128)(2,1)S(1)} %fusion.1), channel_id=1, source_target_pairs={{0,4},{1,5},{2,6},{3,7}} | collective-permute-start | bytes 1179656 | tf_op jit(solution)/shard_map/ppermute | solution.py:478
  5.6 18.4 %collective-permute-start.1 = (bf16[256,768]{1,0:T(8,128)(2,1)S(1)}, bf16[256,768]{1,0:T(8,128)(2,1)}, u32[]{:S(2)}, u32[]{:S(2)}) collective-permute-start(bf16[256,768]{1,0:T(8,128)(2,1)S(1)} %fusion.2), channel_id=1, source_target_pairs={{0,4},{1,5},{2,6},{3,7}} | collective-permute-start | bytes 1179656 | tf_op jit(solution)/shard_map/ppermute | solution.py:479

commit v4 on v3

--- a/solution.py
+++ b/solution.py
@@ -13,7 +13,7 @@
 OUT_ROWS = 256
 UP_TILE = 32
 DOWN_TILE = 512
-EARLY = 14
+EARLY = 12
 OUT_SLOTS = ROWS // OUT_ROWS
 LAG = 4
 DEPTH = 3
@@ -217,7 +217,9 @@
                     y_stage[j] = (x_ref[part, :].astype(jnp.float32) + total[part, :]).astype(jnp.bfloat16)
                     out_copy(k).start()
 
-        last = tokens // ROWS - 1
+        blocks = tokens // ROWS
+        half = blocks // 2
+        assert blocks == 4
         pass_on(1, 0)
         spread(0)
 
@@ -225,6 +227,10 @@
             @pl.when(c < count)
             def _():
                 pass_on(c, 1)
+
+            @pl.when(c >= 2)
+            def _():
+                block(c - 2, half)
 
             @pl.when(c <= count)
             def _():
@@ -235,7 +241,7 @@
 
             @pl.when(c >= 2)
             def _():
-                block(c - 2, last)
+                block(c - 2, half + 1)
 
             @pl.when(c <= count)
             def _():
@@ -246,7 +252,7 @@
                     block(c - 1, t)
                     return carry
 
-                lax.fori_loop(0, last, part, 0)
+                lax.fori_loop(0, half, part, 0)
 
             @pl.when(c + 1 < count)
             def _():
@@ -265,7 +271,7 @@
         lax.fori_loop(1, count + 2, turn, 0)
         for c in range(count + 2 - LAG, count):
             settle(c)
-        for k in range((last + 1) * OUT_SLOTS - OUT_SLOTS, (last + 1) * OUT_SLOTS):
+        for k in range((blocks - 1) * OUT_SLOTS, blocks * OUT_SLOTS):
             out_copy(k).wait()
 
 

time: 621 us -> 605 us (0.974)
  Pallas kernels: 612 us -> 597 us
    pallas_call x1, Pallas kernels: 586 us -> 571 us  [stream_mlp(): pl.pallas_call(stream_kernel, out_shape=(jax.ShapeDtypeStruct((tokens, mo...]
where the time goes in v4:
time: 605 us
  Pallas kernels  597 us (99%)
    pallas_call x1, Pallas kernels, stream_mlp(): pl.pallas_call(stream_kernel, out_shape=(jax.ShapeDtypeStruct((tokens, mo...  571 us
    pallas_call x1, Pallas kernels, early(): pl.pallas_call(early_kernel, out_shape=(jax.ShapeDtypeStruct(up_w.shape,...  16.1 us
  transfers between devices with their start and end apart: 2, of which 1 were waited for; matrix products, arithmetic and copies ran while one was open for 0% of the time, Pallas kernels for 3%

profile of v4, /device:TPU:4, one launch (start us, length us, event | category | flops | bytes accessed | tf_op | source)
XLA Modules:
  0.0 604.8 jit_solution(4196931809985846350)
XLA Ops:
  1.3 1.5 fusion.1
  2.8 1.3 collective-permute-start
  4.1 1.5 fusion.2
  5.6 1.3 collective-permute-start.1
  7.5 16.1 %shard_map.94 = (f32[768,8192]{1,0:T(8,128)}, f32[8192,768]{1,0:T(8,128)}) custom-call(f32[768,8192]{1,0:T(8,128)} %bitcast.15, f32[768,8192]{1,0:T(8,128)} %bitcast.19, f32[1]{0:T(128)} %bitcast.11.rate_ref), custom_call_target="tpu_custom_call" | custom-call | flops 40000000 | bytes 50000000 | tf_op jit(solution)/shard_map/pallas_call | solution.py:407
  23.6 0.0 collective-permute-done.up_head
  23.6 0.3 collective-permute-done.1.down_head
  24.0 571.0 %shard_map.95 = (bf16[2048,3072]{1,0:T(8,128)(2,1)}, bf16[32,3072,256]{2,1,0:T(8,128)(2,1)}, bf16[32,256,3072]{2,1,0:T(8,128)(2,1)}) custom-call(f32[768,8192]{1,0:T(8,128)} %bitcast.16, f32[768,8192]{1,0:T(8,128)} %bitcast.20, f32[8192,768]{1,0:T(8,128)} %bitcast.22, f32[8192,768]{1,0:T(8,128)} %bitcast.24, f32[1]{0:T(128)} %bitcast.12.rate_ref, ...), custom_call_target="tpu_custom_call" | custom-call | flops 206158430208 | bytes 201326592 | tf_op jit(solution)/shard_map/pallas_call | solution.py:444
  595.0 9.8 %shard_map.96 = (f32[768,8192]{1,0:T(8,128)}, f32[8192,768]{1,0:T(8,128)}, bf16[2048,3072]{1,0:T(8,128)(2,1)}) custom-call(f32[768,8192]{1,0:T(8,128)} %bitcast.17, f32[768,8192]{1,0:T(8,128)} %bitcast.21, f32[8192,768]{1,0:T(8,128)} %bitcast.23, f32[8192,768]{1,0:T(8,128)} %bitcast.25, ...), custom_call_target="tpu_custom_call", output_to_operand_aliasing={{0}: (7, {}), {1}: (8, {})} | custom-call | flops 40000000 | bytes 100000000 | tf_op jit(solution)/shard_map/pallas_call | solution.py:423
Async XLA Ops:
  2.8 20.8 %collective-permute-start = (bf16[768,256]{1,0:T(8,128)(2,1)S(1)}, bf16[768,256]{1,0:T(8,128)(2,1)}, u32[]{:S(2)}, u32[]{:S(2)}) collective-permute-start(bf16[768,256]{1,0:T(8,128)(2,1)S(1)} %fusion.1), channel_id=1, source_target_pairs={{0,4},{1,5},{2,6},{3,7}} | collective-permute-start | bytes 1179656 | tf_op jit(solution)/shard_map/ppermute | solution.py:484
  5.6 18.4 %collective-permute-start.1 = (bf16[256,768]{1,0:T(8,128)(2,1)S(1)}, bf16[256,768]{1,0:T(8,128)(2,1)}, u32[]{:S(2)}, u32[]{:S(2)}) collective-permute-start(bf16[256,768]{1,0:T(8,128)(2,1)S(1)} %fusion.2), channel_id=1, source_target_pairs={{0,4},{1,5},{2,6},{3,7}} | collective-permute-start | bytes 1179656 | tf_op jit(solution)/shard_map/ppermute | solution.py:485
